TPU v7x, 512 devices: a 8x2x16 block of a 8x8x16 slice. The times are simulated.
512 devices in a mesh: members: 2 (over y), band: 32 (over z, core), head: 8 (over x).
Axes of the slice: x: 8, y: 2, z: 16, core: 2. Of those that a mesh axis runs over, the one named last changes fastest.
The devices are a block of a 8x8x16 slice.
Arguments:
- grid_feats: bfloat16 [32768, 1024], P(('members', 'band')), parts along dimension 0, may hold values from -6 to 6
- mesh_feats: bfloat16 [32768, 1024], P(('members', 'band')), parts along dimension 0, may hold values from -6 to 6
- enc_in: bfloat16 [3, 1024, 1024], P(None, 'band', 'head'), may hold values from -0.19921875 to 0.19921875
- enc_out: bfloat16 [1024, 1024], P('head', 'band'), may hold values from -0.1875 to 0.1875
- proc_in: bfloat16 [3, 1024, 1024], P(None, 'band', 'head'), may hold values from -0.19921875 to 0.19921875
- proc_out: bfloat16 [1024, 1024], P('head', 'band'), may hold values from -0.1875 to 0.1875
- ff_up: bfloat16 [1024, 4096], P('band', 'head'), may hold values from -0.1875 to 0.1875
- ff_down: bfloat16 [4096, 1024], P('head', 'band'), may hold values from -0.09375 to 0.09375
- dec_in: bfloat16 [3, 1024, 1024], P(None, 'band', 'head'), may hold values from -0.19921875 to 0.19921875
- dec_out: bfloat16 [1024, 1024], P('head', 'band'), may hold values from -0.1875 to 0.1875
- enc_list: int32 [128, 8], replicated, may hold values from 0 to 127, as said below
- enc_count: int32 [128], replicated, may hold values from 1 to 8
- dec_list: int32 [128, 8], replicated, may hold values from 0 to 127, as said below
- dec_count: int32 [128], replicated, may hold values from 1 to 8
- window_ids: int32 [16384], replicated, may hold values from 0 to 20, never falling along the last dimension, each value on 1 to 1536 neighbouring positions
Outputs:
- grid_out: bfloat16 [32768, 1024], P(('members', 'band', 'head')), parts along dimension 0
There are 2 independent parts, one for each index of `members`. A program takes and returns all parts, laid end to end along the dimension named above; an argument that names none is the same for every part. Nothing has to cross between parts.
Inputs may be any that keep to these rules, and one draw needn't show every extreme that they name: `enc_list`: each row holds distinct block numbers. Every block listed for mesh block m lies in the band of 512 grid points with the same band number as m's band of 512 nodes, or in the band just before or just after it. Only the first enc_count[m] slots of row m of enc_list are used. `dec_list`: each row holds distinct block numbers. Every block listed for grid block g lies in the band of 512 mesh nodes with the same band number as g's band of 512 grid points, or in the band just before or just after it. Only the first dec_count[g] slots of row g of dec_list are used. `window_ids`: never falls along the nodes; each window holds at most 1536 consecutive nodes.
All inputs are finite; a program needn't handle non-finite values.
Results may differ from a plain program's by a relative error of at most 0.02.
Values may be sent and summed in bfloat16 or wider, within the bound.
A program may use at most 64 MiB of HBM per device.

v0:
```python
import jax
import jax.numpy as jnp
from jax import lax
from jax.sharding import Mesh
from jax.sharding import PartitionSpec as P

HD = 64
BLOCK = 128
WINDOW = 1536
BAND = ("band_0", "band_1")
MEMBERS_BAND = ("members", "band_0", "band_1")
MEMBERS_BAND_HEAD = ("members", "band_0", "band_1", "head")
EPSILON = 1e-05
NEGATIVE = -1e30


def joined_along(blocks, dim):
    dims = list(blocks.shape[1:])
    dims[dim] *= blocks.shape[0]
    return jnp.moveaxis(blocks, 0, dim).reshape(dims)


def all_blocks(array, axes, order):
    blocks = array[None]
    for k in order:
        blocks = lax.all_gather(blocks, axes[k], axis=0, tiled=True)
    block = [lax.axis_size(axes[k]) for k in reversed(order)]
    blocks = blocks.reshape(*block, *array.shape)
    turned = sorted(range(len(order)), key=lambda place: order[len(order) - 1 - place])
    return blocks.transpose(*turned, *range(len(order), blocks.ndim)).reshape(-1, *array.shape)


def whole_of(array, axes, order, dim):
    return joined_along(all_blocks(array, axes, order), dim)


def padded(block, sides, width):
    for axis, dim in sides:
        count = lax.axis_size(axis)
        forward = [(i, i + 1) for i in range(count - 1)]
        backward = [(target, source) for source, target in forward]
        low = lax.ppermute(
            lax.slice_in_dim(block, block.shape[dim] - width, None, axis=dim), axis, forward
        )
        high = lax.ppermute(lax.slice_in_dim(block, 0, width, axis=dim), axis, backward)
        block = jnp.concatenate([low, block, high], axis=dim)
    return block


def copy_for_each(array, axis):
    size = lax.axis_size(axis)
    return lax.all_to_all(
        jnp.broadcast_to(array[None], (size, *array.shape)), axis, 0, 0, tiled=True
    )


def gathered_copies(array, axis, dim):
    return joined_along(copy_for_each(array, axis), dim)


def shifted(block, axis, distance):
    devices = range(lax.axis_size(axis))
    route = [(i - distance, i) for i in devices if i - distance in devices]
    return lax.ppermute(block, axis, route)


def split_up(array, dim, size):
    dims = array.shape
    blocks = array.reshape(*dims[:dim], size, dims[dim] // size, *dims[dim + 1 :])
    return jnp.moveaxis(blocks, dim, 0)


def summed_on_arrival(array, axis, dim):
    size = lax.axis_size(axis)
    blocks = lax.all_to_all(split_up(array, dim, size), axis, 0, 0, tiled=True)
    return jnp.sum(blocks.astype(jnp.float32), axis=0)


def normed(source):
    values_f = source.astype(jnp.float32)
    centred = values_f - jnp.mean(values_f, axis=-1, keepdims=True)
    variance = jnp.mean(centred * centred, axis=-1, keepdims=True)
    return (centred * lax.rsqrt(variance + EPSILON)).astype(jnp.bfloat16)


def fold_three(sources, carry, piece):
    width = piece.shape[1]
    return tuple(
        (
            total
            + jnp.dot(
                lax.slice_in_dim(source, 0, width, axis=1),
                piece[which],
                preferred_element_type=jnp.float32,
            )
            for which, (total, source) in enumerate(zip(carry, sources))
        )
    )


def fold_rows(source, total, piece):
    return total + jnp.dot(
        lax.slice_in_dim(source, 0, piece.shape[0], axis=1),
        piece,
        preferred_element_type=jnp.float32,
    )


def columns_of(source, piece):
    return jnp.dot(source, piece, preferred_element_type=jnp.float32)


def head_scores(queries, key_rows, head_index, allowed):
    lower = head_index * HD
    scores = jnp.einsum(
        "qd,kd->qk",
        queries[:, lower : lower + HD],
        key_rows[:, lower : lower + HD],
        preferred_element_type=jnp.float32,
    ) * HD ** (-0.5)
    scores = jnp.where(allowed, scores, NEGATIVE)
    maxima = jnp.max(scores, axis=1, keepdims=True)
    expo = jnp.where(allowed, jnp.exp(scores - maxima), 0.0)
    return (expo, maxima, jnp.sum(expo, axis=1, keepdims=True))


def attend_rounded(queries, key_rows, value_rows, allowed):
    outputs = []
    for head_index in range(queries.shape[1] // HD):
        expo, maxima, totals = head_scores(queries, key_rows, head_index, allowed)
        weights = (expo / totals).astype(jnp.bfloat16)
        lower = head_index * HD
        outputs.append(
            jnp.dot(weights, value_rows[:, lower : lower + HD], preferred_element_type=jnp.float32)
        )
    return jnp.concatenate(outputs, axis=1).astype(jnp.bfloat16)


def partial_attend(queries, key_rows, value_rows, allowed):
    outputs, maxima_all, totals_all = ([], [], [])
    for head_index in range(queries.shape[1] // HD):
        expo, maxima, totals = head_scores(queries, key_rows, head_index, allowed)
        lower = head_index * HD
        outputs.append(jnp.dot(expo, value_rows[:, lower : lower + HD].astype(jnp.float32)))
        maxima_all.append(maxima)
        totals_all.append(totals)
    return (
        jnp.concatenate(outputs, axis=1),
        jnp.concatenate(maxima_all, axis=1),
        jnp.concatenate(totals_all, axis=1),
    )


def listed_attend(queries, key_pool, value_pool, lists, counts, base_block, rounded):
    width = queries.shape[1]
    rows = queries.shape[0]
    pool_blocks = key_pool.shape[0] // BLOCK
    key_blocks = key_pool.reshape(pool_blocks, BLOCK, width)
    value_blocks = value_pool.reshape(pool_blocks, BLOCK, width)
    slots = lists.shape[1]

    def one_block(index):
        listed = lists[index] - base_block
        inside = (
            (listed >= 0)
            & (listed < pool_blocks)
            & (jnp.arange(slots, dtype=jnp.int32) < counts[index])
        )
        safe = jnp.clip(listed, 0, pool_blocks - 1)
        block_keys = key_blocks[safe].reshape(slots * BLOCK, width)
        block_values = value_blocks[safe].reshape(slots * BLOCK, width)
        allowed = jnp.repeat(inside, BLOCK)[None, :]
        block_queries = lax.dynamic_slice_in_dim(queries, index * BLOCK, BLOCK, 0)
        if rounded:
            return attend_rounded(block_queries, block_keys, block_values, allowed)
        return partial_attend(block_queries, block_keys, block_values, allowed)

    result = lax.map(one_block, jnp.arange(rows // BLOCK, dtype=jnp.int32))
    return jax.tree.map(lambda stacked: stacked.reshape(rows, stacked.shape[-1]), result)


def normalize(outputs, totals):
    rows = outputs.shape[0]
    heads_here = totals.shape[1]
    shaped = outputs.reshape(rows, heads_here, HD) / totals[:, :, None]
    return shaped.reshape(rows, heads_here * HD).astype(jnp.bfloat16)


def per_device(
    grid_feats,
    mesh_feats,
    enc_in,
    enc_out,
    proc_in,
    proc_out,
    ff_up,
    ff_down,
    dec_in,
    dec_out,
    enc_list,
    enc_count,
    dec_list,
    dec_count,
    window_ids,
):
    band_index = lax.axis_index(BAND)
    grid_rows = grid_feats.shape[0]
    mesh_rows = mesh_feats.shape[0]
    width = enc_in.shape[2]
    grid_blocks = grid_rows // BLOCK
    mesh_blocks = mesh_rows // BLOCK
    grid_norm = normed(grid_feats)
    mesh_norm = normed(mesh_feats)
    grid_zeros = jnp.zeros((grid_rows, width), jnp.float32)
    mesh_zeros = jnp.zeros((mesh_rows, width), jnp.float32)
    enc_q, enc_k, enc_v = fold_three(
        (mesh_norm, grid_norm, grid_norm),
        (mesh_zeros, grid_zeros, grid_zeros),
        whole_of(enc_in, BAND, (0, 1), 1),
    )
    enc_q = enc_q.astype(jnp.bfloat16)
    enc_k = enc_k.astype(jnp.bfloat16)
    enc_v = enc_v.astype(jnp.bfloat16)
    my_lists = lax.dynamic_slice_in_dim(enc_list, band_index * mesh_blocks, mesh_blocks, 0)
    my_counts = lax.dynamic_slice_in_dim(enc_count, band_index * mesh_blocks, mesh_blocks, 0)
    pool = padded(jnp.stack([enc_k, enc_v]), ((BAND, 1),), grid_rows)
    outputs, maxima, totals = listed_attend(
        enc_q, pool[0], pool[1], my_lists, my_counts, (band_index - 1) * grid_blocks, False
    )
    enc_attn = normalize(outputs, totals)
    enc_terms = columns_of(enc_attn, gathered_copies(enc_out, BAND, 1))
    mesh_state = mesh_feats.astype(jnp.float32) + lax.psum(
        enc_terms.astype(jnp.bfloat16), "head"
    ).astype(jnp.float32)
    proc_norm = normed(mesh_state)
    proc_q, proc_k, proc_v = fold_three(
        (proc_norm, proc_norm, proc_norm),
        (mesh_zeros, mesh_zeros, mesh_zeros),
        whole_of(proc_in, BAND, (0, 1), 1),
    )
    proc_q = proc_q.astype(jnp.bfloat16)
    pairs = jnp.stack([proc_k.astype(jnp.bfloat16), proc_v.astype(jnp.bfloat16)])
    reach = (WINDOW + mesh_rows - 2) // mesh_rows
    slab_parts = {0: pairs}
    for distance in range(1, reach + 1):
        for direction in (1, -1):
            slab_parts[direction * distance] = shifted(pairs, BAND, -direction * distance)
    slab = jnp.concatenate([slab_parts[offset] for offset in range(-reach, reach + 1)], axis=1)
    padded_ids = jnp.pad(window_ids, (reach * mesh_rows, reach * mesh_rows), constant_values=-1)
    slab_ids = lax.dynamic_slice_in_dim(
        padded_ids, band_index * mesh_rows, (2 * reach + 1) * mesh_rows, 0
    )
    slab_start = (band_index - reach) * mesh_rows
    span = 2 * WINDOW

    def window_block(index):
        first = band_index * mesh_rows + index * BLOCK
        first_id = window_ids[first]
        window_start = jnp.sum((window_ids < first_id).astype(jnp.int32))
        local = window_start - slab_start
        block_keys = lax.dynamic_slice_in_dim(slab[0], local, span, 0)
        block_values = lax.dynamic_slice_in_dim(slab[1], local, span, 0)
        key_ids = lax.dynamic_slice_in_dim(slab_ids, local, span, 0)
        query_ids = lax.dynamic_slice_in_dim(window_ids, first, BLOCK, 0)
        block_queries = lax.dynamic_slice_in_dim(proc_q, index * BLOCK, BLOCK, 0)
        return attend_rounded(
            block_queries, block_keys, block_values, query_ids[:, None] == key_ids[None, :]
        )

    proc_attn = lax.map(window_block, jnp.arange(mesh_blocks, dtype=jnp.int32)).reshape(
        mesh_rows, width
    )
    proc_terms = columns_of(proc_attn, gathered_copies(proc_out, BAND, 1))
    mesh_mid = mesh_state + lax.psum(proc_terms.astype(jnp.bfloat16), "head").astype(jnp.float32)
    ff_norm = normed(mesh_mid)
    hidden = fold_rows(
        ff_norm,
        jnp.zeros((mesh_rows, ff_up.shape[1]), jnp.float32),
        whole_of(ff_up, BAND, (0, 1), 0),
    )
    hidden = jax.nn.gelu(hidden, approximate=False).astype(jnp.bfloat16)
    ff_terms = columns_of(hidden, whole_of(ff_down, BAND, (0, 1), 1))
    mesh_final = mesh_mid + lax.psum(ff_terms.astype(jnp.bfloat16), "head").astype(jnp.float32)
    final_norm = normed(mesh_final)
    dec_q, dec_k, dec_v = fold_three(
        (grid_norm, final_norm, final_norm),
        (grid_zeros, mesh_zeros, mesh_zeros),
        whole_of(dec_in, BAND, (0, 1), 1),
    )
    dec_q = dec_q.astype(jnp.bfloat16)
    dec_pool = padded(
        jnp.stack([dec_k.astype(jnp.bfloat16), dec_v.astype(jnp.bfloat16)]), ((BAND, 1),), mesh_rows
    )
    grid_lists = lax.dynamic_slice_in_dim(dec_list, band_index * grid_blocks, grid_blocks, 0)
    grid_counts = lax.dynamic_slice_in_dim(dec_count, band_index * grid_blocks, grid_blocks, 0)
    dec_attn = listed_attend(
        dec_q,
        dec_pool[0],
        dec_pool[1],
        grid_lists,
        grid_counts,
        (band_index - 1) * mesh_blocks,
        True,
    )
    full_out = gathered_copies(dec_out, BAND, 1)
    share = grid_rows // lax.axis_size("head")
    summed = summed_on_arrival(
        jnp.dot(
            lax.slice_in_dim(dec_attn, 0, share * lax.axis_size("head"), axis=0),
            full_out,
            preferred_element_type=jnp.float32,
        ).astype(jnp.bfloat16),
        "head",
        0,
    )
    residual = lax.dynamic_slice_in_dim(
        grid_feats, lax.axis_index("head") * share, share, 0
    ).astype(jnp.float32)
    return (residual + summed).astype(jnp.bfloat16)


def solution(mesh):
    finer = Mesh(
        mesh.devices.reshape(mesh.shape["members"], 16, 2, mesh.shape["head"]),
        ("members", "band_0", "band_1", "head"),
    )
    placed = (
        P(MEMBERS_BAND, None),
        P(MEMBERS_BAND, None),
        P(None, BAND, "head"),
        P("head", BAND),
        P(None, BAND, "head"),
        P("head", BAND),
        P(BAND, "head"),
        P("head", BAND),
        P(None, BAND, "head"),
        P("head", BAND),
        P(),
        P(),
        P(),
        P(),
        P(),
    )
    return jax.shard_map(
        per_device,
        mesh=finer,
        in_specs=placed,
        out_specs=P(MEMBERS_BAND_HEAD, None),
        check_vma=False,
    )
```

profile of v0, /device:TPU:65, one launch (start us, length us, event | category | flops | bytes accessed | tf_op | source)
XLA Modules:
  0.0 632.4 jit_solution(11155338328643831637)
XLA Ops:
  10.9 64.3 %all-gather.1 = bf16[48,32,128]{2,1,0:T(8,128)(2,1)S(1)} all-gather(bf16[3,32,128]{2,1,0:T(8,128)(2,1)S(1)} %copy-done.15), channel_id=3, replica_groups=mesh['members'=2,'band_0'=16,'band_1'=2,'head'=8] {'band_0'}, dimensions={0}, use_global_device_ids=true | all-gather | bytes 417792 | tf_op jit(solution)/shard_map/all_gather | solution.py:26
  75.2 9.4 %all_gather.33 = bf16[32,3,32,128]{3,2,1,0:T(8,128)(2,1)S(1)} all-gather(bf16[16,3,32,128]{3,2,1,0:T(8,128)(2,1)S(1)} %bitcast.225), channel_id=1, replica_groups=mesh['members'=2,'band_0'=16,'band_1'=2,'head'=8] {'band_1'}, dimensions={0}, use_global_device_ids=true | all-gather | bytes 1179648 | tf_op jit(solution)/shard_map/all_gather | solution.py:26
  88.1 3.3 collective-permute-start
  92.2 4.8 all-to-all-start
  100.3 39.7 %while.34 = (s32[]{:T(128)}, f32[4,128,128]{2,1,0:T(8,128)}, f32[4,128,2]{1,2,0:T(2,128)}, s32[4]{0:T(128)}, s32[4,8]{1,0:T(4,128)S(1)}, /*index=5*/s32[]{:T(128...) while((s32[]{:T(128)}, f32[4,128,128]{2,1,0:T(8,128)}, ...), condition=%wide.region_9.10_spmd, body=%wide.region_4.9_spmd.sunk | while | flops 69223264 | bytes 5784073 | solution.py:178
  144.5 24.8 %all-gather.4 = bf16[8192,32]{0,1:T(8,128)(2,1)S(1)} all-gather(bf16[512,32]{0,1:T(8,128)(2,1)S(1)} %copy-done.13), channel_id=6, replica_groups=mesh['members'=2,'band_0'=16,'band_1'=2,'head'=8] {'band_0'}, dimensions={0}, use_global_device_ids=true | all-gather | bytes 557056 | tf_op jit(solution)/shard_map/all_gather | solution.py:26
  171.1 16.2 %all-to-all-start.1 = ((bf16[32,128,32]{1,2,0:T(8,128)(2,1)}), bf16[32,128,32]{1,2,0:T(8,128)(2,1)S(1)}, u32[]{:S(2)}, u32[]{:S(2)}) async-start(bf16[32,128,32]{1,2,0:T(8,128)(2,1)} %broadcast_in_dim.159), calls=%async_computation.1 | async-start | bytes 524288 | tf_op jit(solution)/shard_map/all_to_all | solution.py:52
  187.4 37.6 %all-gather.3 = bf16[512,512]{1,0:T(8,128)(2,1)} all-gather(bf16[32,512]{1,0:T(8,128)(2,1)S(1)} %copy-done.14), channel_id=5, replica_groups=mesh['members'=2,'band_0'=16,'band_1'=2,'head'=8] {'band_0'}, dimensions={0}, use_global_device_ids=true | all-gather | bytes 557056 | tf_op jit(solution)/shard_map/all_gather | solution.py:26
  225.1 23.3 %all-gather.2 = bf16[48,32,128]{2,1,0:T(8,128)(2,1)S(1)} all-gather(bf16[3,32,128]{2,1,0:T(8,128)(2,1)S(1)} %copy-done.16), channel_id=4, replica_groups=mesh['members'=2,'band_0'=16,'band_1'=2,'head'=8] {'band_0'}, dimensions={0}, use_global_device_ids=true | all-gather | bytes 417792 | tf_op jit(solution)/shard_map/all_gather | solution.py:26
  248.4 13.6 %all_gather.35 = bf16[32,3,32,128]{3,2,1,0:T(8,128)(2,1)S(1)} all-gather(bf16[16,3,32,128]{3,2,1,0:T(8,128)(2,1)S(1)} %bitcast.226), channel_id=1, replica_groups=mesh['members'=2,'band_0'=16,'band_1'=2,'head'=8] {'band_1'}, dimensions={0}, use_global_device_ids=true | all-gather | bytes 1179648 | tf_op jit(solution)/shard_map/all_gather | solution.py:26
  265.8 4.0 collective-permute-start.2
  269.9 3.3 collective-permute-start.3
  288.0 10.1 %collective-permute-done.7 = bf16[2,512,128]{2,1,0:T(8,128)(2,1)S(1)} collective-permute-done((bf16[2,512,128]{2,1,0:T(8,128)(2,1)S(1)}, bf16[2,512,128]{2,1,0:T(8,128)(2,1)S(1)}, u32[]{:S(2)}, u32[]{:S(2)}) %collective-permute-start.7) | collective-permute-done | bytes 262176 | tf_op jit(solution)/shard_map/ppermute | solution.py:64
  299.4 49.0 %while.35 = (s32[]{:T(128)}, bf16[4,128,128]{2,1,0:T(8,128)(2,1)S(1)}, s32[4]{0:T(128)S(1)}, s32[]{:T(128)}, s32[16384]{0:T(1024)S(1)}, /*index=5*/s32[]{:T(128)...) while((s32[]{:T(128)}, ...), condition=%wide.region_19.20_spmd, body=%wide.region_13.19_spmd.sunk | while | flops 211287568 | bytes 26145704 | solution.py:270
  355.3 77.1 %all-reduce.7.cloned.1.call-done = bf16[512,1024]{1,0:T(8,128)(2,1)} async-done(((bf16[512,1024]{1,0:T(8,128)(2,1)}), bf16[512,1024]{1,0:T(8,128)(2,1)}) %all-reduce.7.cloned.1.call-update) | async-done | bytes 1048592 | tf_op jit(solution)/shard_map/psum | solution.py:274
  435.7 5.6 convolution_convert_fusion.7
  441.4 26.9 %all-gather = bf16[48,32,128]{2,1,0:T(8,128)(2,1)S(1)} all-gather(bf16[3,32,128]{2,1,0:T(8,128)(2,1)S(1)} %copy-done.17), channel_id=2, replica_groups=mesh['members'=2,'band_0'=16,'band_1'=2,'head'=8] {'band_0'}, dimensions={0}, use_global_device_ids=true | all-gather | bytes 417792 | tf_op jit(solution)/shard_map/all_gather | solution.py:26
  468.3 14.2 %all_gather.31 = bf16[32,3,32,128]{3,2,1,0:T(8,128)(2,1)S(1)} all-gather(bf16[16,3,32,128]{3,2,1,0:T(8,128)(2,1)S(1)} %bitcast.227), channel_id=1, replica_groups=mesh['members'=2,'band_0'=16,'band_1'=2,'head'=8] {'band_1'}, dimensions={0}, use_global_device_ids=true | all-gather | bytes 1179648 | tf_op jit(solution)/shard_map/all_gather | solution.py:26
  483.4 45.9 %all-reduce.9.cloned.1.call-done = bf16[512,1024]{1,0:T(8,128)(2,1)} async-done(((bf16[512,1024]{1,0:T(8,128)(2,1)}), bf16[512,1024]{1,0:T(8,128)(2,1)}) %all-reduce.9.cloned.1.call-update) | async-done | bytes 1048592 | tf_op jit(solution)/shard_map/psum | solution.py:283
  533.3 7.6 %collective-permute-start.9 = (bf16[2,512,128]{2,1,0:T(8,128)(2,1)S(1)}, bf16[2,512,128]{2,1,0:T(8,128)(2,1)S(1)}, u32[]{:S(2)}, u32[]{:S(2)}) collective-permute-start(bf16[2,512,128]{2,1,0:T(8,128)(2,1)S(1)} %pad_maximum_fusion.6), channel_id=1, source_target_pairs={{8,0},{16,8},{24,16},{32,24},{40,32},{48,40},{56,48},{64,56},{72,6... | collective-permute-start | bytes 786440 | tf_op jit(solution)/shard_map/ppermute | solution.py:45
  544.8 12.4 %all-to-all-start.2 = ((bf16[32,128,32]{1,2,0:T(8,128)(2,1)}), bf16[32,128,32]{1,2,0:T(8,128)(2,1)S(1)}, u32[]{:S(2)}, u32[]{:S(2)}) async-start(bf16[32,128,32]{1,2,0:T(8,128)(2,1)} %broadcast_in_dim.162), calls=%async_computation.2 | async-start | bytes 524288 | tf_op jit(solution)/shard_map/all_to_all | solution.py:52
  558.0 30.9 %while.36 = (s32[]{:T(128)}, bf16[4,128,128]{2,1,0:T(8,128)(2,1)S(1)}, s32[4]{0:T(128)S(1)}, s32[4,8]{1,0:T(4,128)S(1)}, s32[]{:T(128)}, /*index=5*/s32[4]{0:T(1...) while((s32[]{:T(128)}, ...), condition=%wide.region_31.32_spmd, body=%wide.region_26.31_spmd.sunk | while | flops 69812832 | bytes 5553661 | solution.py:178
  590.4 3.9 all-to-all-start.3
  594.3 29.2 %all-to-all-done.3 = bf16[8,64,1024]{2,1,0:T(8,128)(2,1)S(1)} async-done(((bf16[8,64,1024]{2,1,0:T(8,128)(2,1)}), bf16[8,64,1024]{2,1,0:T(8,128)(2,1)S(1)}, u32[]{:S(2)}, u32[]{:S(2)}) %all-to-all-start.3) | async-done | bytes 1048608 | tf_op jit(solution)/shard_map/all_to_all | solution.py:75
  (367 shorter events, 153.2 us)
Async XLA Ops:
  10.9 74.3 %copy-start.5 = (bf16[512,1024]{1,0:T(8,128)(2,1)}, bf16[512,1024]{1,0:T(8,128)(2,1)S(1)}, u32[]{:S(2)}) copy-start(bf16[512,1024]{1,0:T(8,128)(2,1)S(1)} %fusion.65) | copy-start | bytes 3145732
  85.8 13.8 %collective-permute-start.1 = (bf16[2,512,128]{2,1,0:T(8,128)(2,1)S(1)}, bf16[2,512,128]{2,1,0:T(8,128)(2,1)S(1)}, u32[]{:S(2)}, u32[]{:S(2)}) collective-permute-start(bf16[2,512,128]{2,1,0:T(8,128)(2,1)S(1)} %pad_maximum_fusion.4), channel_id=1, source_target_pairs={{8,0},{16,8},{24,16},{32,24},{40,32},{48,40},{56,48},{64,56},{72,6... | collective-permute-start | bytes 786440 | tf_op jit(solution)/shard_map/ppermute | solution.py:45
  88.1 11.5 %collective-permute-start = (bf16[2,512,128]{2,1,0:T(8,128)(2,1)S(1)}, bf16[2,512,128]{2,1,0:T(8,128)(2,1)S(1)}, u32[]{:S(2)}, u32[]{:S(2)}) collective-permute-start(bf16[2,512,128]{2,1,0:T(8,128)(2,1)S(1)} %pad_maximum_fusion.4), channel_id=1, source_target_pairs={{0,8},{8,16},{16,24},{24,32},{32,40},{40,48},{48,56},{56,64},{64,7... | collective-permute-start | bytes 786440 | tf_op jit(solution)/shard_map/ppermute | solution.py:42
  92.2 49.8 %all-to-all-start = ((bf16[32,128,32]{1,2,0:T(8,128)(2,1)}), bf16[32,128,32]{1,2,0:T(8,128)(2,1)}, u32[]{:S(2)}, u32[]{:S(2)}) async-start(bf16[32,128,32]{1,2,0:T(8,128)(2,1)} %broadcast_in_dim.157), calls=%async_computation | async-start | bytes 524288 | tf_op jit(solution)/shard_map/all_to_all | solution.py:52
  97.0 165.2 %all-reduce.5.cloned.1.call-start = ((), (), s32[]{:S(2)}) async-start(), calls=%async_computation.4 | async-start | bytes 2097152 | tf_op jit(solution)/shard_map/psum | solution.py:232
  144.3 26.0 %copy-start.20 = (bf16[128,32]{0,1:T(8,128)(2,1)S(1)}, bf16[128,32]{0,1:T(8,128)(2,1)}, u32[]{:S(2)}) copy-start(bf16[128,32]{0,1:T(8,128)(2,1)} %param.26) | copy-start | bytes 24580
  144.3 43.0 %copy-start.14 = (bf16[32,512]{1,0:T(8,128)(2,1)S(1)}, bf16[32,512]{1,0:T(8,128)(2,1)}, u32[]{:S(2)}) copy-start(bf16[32,512]{1,0:T(8,128)(2,1)} %param.27) | copy-start | bytes 98308
  144.4 205.8 %all-gather.10.cloned.1.call-start = ((), (), s32[]{:S(2)}) async-start(), calls=%async_computation.7 | async-start | bytes 1572864 | tf_op jit(solution)/shard_map/all_gather | solution.py:26
  169.3 55.8 %copy-start.16 = (bf16[3,32,128]{2,1,0:T(8,128)(2,1)S(1)}, bf16[3,32,128]{2,1,0:T(8,128)(2,1)}, u32[]{:S(2)}) copy-start(bf16[3,32,128]{2,1,0:T(8,128)(2,1)} %param.25) | copy-start | bytes 73732
  171.1 177.3 %all-to-all-start.1 = ((bf16[32,128,32]{1,2,0:T(8,128)(2,1)}), bf16[32,128,32]{1,2,0:T(8,128)(2,1)S(1)}, u32[]{:S(2)}, u32[]{:S(2)}) async-start(bf16[32,128,32]{1,2,0:T(8,128)(2,1)} %broadcast_in_dim.159), calls=%async_computation.1 | async-start | bytes 524288 | tf_op jit(solution)/shard_map/all_to_all | solution.py:52
  187.3 165.7 %all-gather.8.cloned.1.call-start = ((), (), s32[]{:S(2)}) async-start(), calls=%async_computation.6 | async-start | bytes 1572864 | tf_op jit(solution)/shard_map/all_gather | solution.py:26
  225.0 207.4 %all-reduce.7.cloned.1.call-start = ((), (), s32[]{:S(2)}) async-start(), calls=%async_computation.5 | async-start | bytes 2097152 | tf_op jit(solution)/shard_map/psum | solution.py:274
  265.8 13.7 %collective-permute-start.2 = (bf16[2,512,128]{2,1,0:T(8,128)(2,1)S(1)}, bf16[2,512,128]{2,1,0:T(8,128)(2,1)}, u32[]{:S(2)}, u32[]{:S(2)}) collective-permute-start(bf16[2,512,128]{2,1,0:T(8,128)(2,1)S(1)} %pad_maximum_fusion.5), channel_id=1, source_target_pairs={{0,24},{8,32},{16,40},{24,48},{32,56},{40,64},{48,72},{56,80},{64,... | collective-permute-start | bytes 786440 | tf_op jit(solution)/shard_map/ppermute | solution.py:64
  269.9 11.8 %collective-permute-start.3 = (bf16[2,512,128]{2,1,0:T(8,128)(2,1)S(1)}, bf16[2,512,128]{2,1,0:T(8,128)(2,1)S(1)}, u32[]{:S(2)}, u32[]{:S(2)}) collective-permute-start(bf16[2,512,128]{2,1,0:T(8,128)(2,1)S(1)} %pad_maximum_fusion.5), channel_id=1, source_target_pairs={{0,16},{8,24},{16,32},{24,40},{32,48},{40,56},{48,64},{56,72},{64,... | collective-permute-start | bytes 786440 | tf_op jit(solution)/shard_map/ppermute | solution.py:64
  273.2 10.5 %collective-permute-start.4 = (bf16[2,512,128]{2,1,0:T(8,128)(2,1)S(1)}, bf16[2,512,128]{2,1,0:T(8,128)(2,1)S(1)}, u32[]{:S(2)}, u32[]{:S(2)}) collective-permute-start(bf16[2,512,128]{2,1,0:T(8,128)(2,1)S(1)} %pad_maximum_fusion.5), channel_id=1, source_target_pairs={{0,8},{8,16},{16,24},{24,32},{32,40},{40,48},{48,56},{56,64},{64,7... | collective-permute-start | bytes 786440 | tf_op jit(solution)/shard_map/ppermute | solution.py:64
  275.7 9.1 %collective-permute-start.5 = (bf16[2,512,128]{2,1,0:T(8,128)(2,1)S(1)}, bf16[2,512,128]{2,1,0:T(8,128)(2,1)S(1)}, u32[]{:S(2)}, u32[]{:S(2)}) collective-permute-start(bf16[2,512,128]{2,1,0:T(8,128)(2,1)S(1)} %pad_maximum_fusion.5), channel_id=1, source_target_pairs={{8,0},{16,8},{24,16},{32,24},{40,32},{48,40},{56,48},{64,56},{72,6... | collective-permute-start | bytes 786440 | tf_op jit(solution)/shard_map/ppermute | solution.py:64
  277.7 10.2 %collective-permute-start.6 = (bf16[2,512,128]{2,1,0:T(8,128)(2,1)S(1)}, bf16[2,512,128]{2,1,0:T(8,128)(2,1)S(1)}, u32[]{:S(2)}, u32[]{:S(2)}) collective-permute-start(bf16[2,512,128]{2,1,0:T(8,128)(2,1)S(1)} %pad_maximum_fusion.5), channel_id=1, source_target_pairs={{16,0},{24,8},{32,16},{40,24},{48,32},{56,40},{64,48},{72,56},{80,... | collective-permute-start | bytes 786440 | tf_op jit(solution)/shard_map/ppermute | solution.py:64
  279.4 18.6 %collective-permute-start.7 = (bf16[2,512,128]{2,1,0:T(8,128)(2,1)S(1)}, bf16[2,512,128]{2,1,0:T(8,128)(2,1)S(1)}, u32[]{:S(2)}, u32[]{:S(2)}) collective-permute-start(bf16[2,512,128]{2,1,0:T(8,128)(2,1)S(1)} %pad_maximum_fusion.5), channel_id=1, source_target_pairs={{24,0},{32,8},{40,16},{48,24},{56,32},{64,40},{72,48},{80,56},{88,... | collective-permute-start | bytes 786440 | tf_op jit(solution)/shard_map/ppermute | solution.py:64
  349.9 179.4 %all-reduce.9.cloned.1.call-start = ((), (), s32[]{:S(2)}) async-start(), calls=%async_computation.8 | async-start | bytes 2097152 | tf_op jit(solution)/shard_map/psum | solution.py:283
  532.3 25.1 %copy-start.6 = (bf16[512,1024]{1,0:T(8,128)(2,1)S(1)}, bf16[512,1024]{1,0:T(8,128)(2,1)}, u32[]{:S(2)}) copy-start(bf16[512,1024]{1,0:T(8,128)(2,1)} %copy-done.5) | copy-start | bytes 3145732
  533.3 24.6 %collective-permute-start.9 = (bf16[2,512,128]{2,1,0:T(8,128)(2,1)S(1)}, bf16[2,512,128]{2,1,0:T(8,128)(2,1)S(1)}, u32[]{:S(2)}, u32[]{:S(2)}) collective-permute-start(bf16[2,512,128]{2,1,0:T(8,128)(2,1)S(1)} %pad_maximum_fusion.6), channel_id=1, source_target_pairs={{8,0},{16,8},{24,16},{32,24},{40,32},{48,40},{56,48},{64,56},{72,6... | collective-permute-start | bytes 786440 | tf_op jit(solution)/shard_map/ppermute | solution.py:45
  540.9 17.0 %collective-permute-start.8 = (bf16[2,512,128]{2,1,0:T(8,128)(2,1)S(1)}, bf16[2,512,128]{2,1,0:T(8,128)(2,1)S(1)}, u32[]{:S(2)}, u32[]{:S(2)}) collective-permute-start(bf16[2,512,128]{2,1,0:T(8,128)(2,1)S(1)} %pad_maximum_fusion.6), channel_id=1, source_target_pairs={{0,8},{8,16},{16,24},{24,32},{32,40},{40,48},{48,56},{56,64},{64,7... | collective-permute-start | bytes 786440 | tf_op jit(solution)/shard_map/ppermute | solution.py:42
  544.8 44.1 %all-to-all-start.2 = ((bf16[32,128,32]{1,2,0:T(8,128)(2,1)}), bf16[32,128,32]{1,2,0:T(8,128)(2,1)S(1)}, u32[]{:S(2)}, u32[]{:S(2)}) async-start(bf16[32,128,32]{1,2,0:T(8,128)(2,1)} %broadcast_in_dim.162), calls=%async_computation.2 | async-start | bytes 524288 | tf_op jit(solution)/shard_map/all_to_all | solution.py:52
  590.4 33.1 %all-to-all-start.3 = ((bf16[8,64,1024]{2,1,0:T(8,128)(2,1)}), bf16[8,64,1024]{2,1,0:T(8,128)(2,1)S(1)}, u32[]{:S(2)}, u32[]{:S(2)}) async-start(bf16[8,64,1024]{2,1,0:T(8,128)(2,1)} %bitcast.85), calls=%async_computation.3 | async-start | bytes 2097152 | tf_op jit(solution)/shard_map/all_to_all | solution.py:75
  (27 other events, 158.1 us)
Sparse Core Ops, SparseCore 0:
  144.5 84.8 all-reduce.4
  350.0 82.4 all-reduce.6
  441.5 87.7 all-reduce.8
Sparse Core Ops, SparseCore 1:
  170.4 29.2 all-gather.9
  225.1 29.3 all-gather.7
where the time goes:
time: 635 us; the launch traced here: 632 us
  blocking collectives  214 us (34%)
  waiting for transfers between devices  169 us (27%)
  starting transfers between devices  68.7 us (11%)
  local copies, waits for them, and re-layouts  64.8 us (10%)
  matrix products  41.6 us (7%)
  other arithmetic  33 us (5%)
  loops' own time  26.2 us (4%)
  between operations  15.4 us (2%)
    all_gather x8, blocking collectives, all_blocks(): blocks = lax.all_gather(blocks, axes[k], axis=0, tiled=True)  214 us
    psum x1, waiting for transfers between devices, per_device(): lax.psum(proc_terms.astype(jnp.bfloat16), 'head').astype(jnp.float32)  77.1 us
    psum x1, waiting for transfers between devices, per_device(): lax.psum(ff_terms.astype(jnp.bfloat16), 'head').astype(jnp.float32)  45.9 us
    all_to_all x3, starting transfers between devices, copy_for_each(): lax.all_to_all(jnp.broadcast_to(array[None], (size, *array.shape)), axis,...  33.5 us
    all_to_all x1, waiting for transfers between devices, summed_on_arrival(): blocks = lax.all_to_all(split_up(array, dim, size), axis, 0, 0, tiled=True)  29.2 us
    another operation x2, loops' own time, listed_attend(): result = lax.map(one_block, jnp.arange(rows // BLOCK, dtype=jnp.int32))  20.8 us
    ppermute x6, waiting for transfers between devices, shifted(): return lax.ppermute(block, axis, route)  16.1 us
    dot_general x24, matrix products, head_scores(): jnp.einsum('qd,kd->qk', queries[:, lower:lower + HD], key_rows[:, lower:l...  15 us
  transfers between devices with their start and end apart: 19, of which 7 were waited for; matrix products, arithmetic and copies ran while one was open for 18% of the time, Pallas kernels for 0%

commit v1 on v0

--- a/solution.py
+++ b/solution.py
@@ -23,7 +23,9 @@
 def all_blocks(array, axes, order):
     blocks = array[None]
     for k in order:
-        blocks = lax.all_gather(blocks, axes[k], axis=0, tiled=True)
+        blocks = jnp.concatenate(
+            lax.all_to_all(jnp.stack([blocks] * lax.axis_size(axes[k])), axes[k], 0, 0), axis=0
+        )
     block = [lax.axis_size(axes[k]) for k in reversed(order)]
     blocks = blocks.reshape(*block, *array.shape)
     turned = sorted(range(len(order)), key=lambda place: order[len(order) - 1 - place])

time: 635 us -> 664 us (1.046)
  blocking collectives: 214 us -> 25 us
  waiting for transfers between devices: 169 us -> 274 us
  starting transfers between devices: 68.7 us -> 165 us
  local copies, waits for them, and re-layouts: 64.8 us -> 74.5 us
    all_gather x8 -> x0, blocking collectives: 214 us -> none  [all_blocks(): blocks = lax.all_gather(blocks, axes[k], axis=0, tiled=True)]
    all_to_all x0 -> x7, starting transfers between devices: none -> 93.1 us  [all_blocks(): lax.all_to_all(jnp.stack([blocks] * lax.axis_size(axes[k])), axes[k], 0, 0)]
    psum x1, waiting for transfers between devices: 0.02 us -> 66.1 us  [per_device(): lax.psum(enc_terms.astype(jnp.bfloat16), 'head').astype(jnp.float32)]
    psum x1, waiting for transfers between devices: 45.9 us -> 77.1 us  [per_device(): lax.psum(ff_terms.astype(jnp.bfloat16), 'head').astype(jnp.float32)]
    all_to_all x0 -> x3, blocking collectives: none -> 25 us  [all_blocks(): lax.all_to_all(jnp.stack([blocks] * lax.axis_size(axes[k])), axes[k], 0, 0)]
    psum x1, waiting for transfers between devices: 77.1 us -> 53.4 us  [per_device(): lax.psum(proc_terms.astype(jnp.bfloat16), 'head').astype(jnp.float32)]
    all_to_all x0 -> x7, waiting for transfers between devices: none -> 16.9 us  [all_blocks(): lax.all_to_all(jnp.stack([blocks] * lax.axis_size(axes[k])), axes[k], 0, 0)]
    ppermute x2, waiting for transfers between devices: 0.01 us -> 7.83 us  [padded(): lax.ppermute(lax.slice_in_dim(block, 0, width, axis=dim), axis, backward)]
  transfers between devices with their start and end apart: 19 -> 24, of which waited for: 7 -> 12; matrix products, arithmetic and copies ran while one was open for 18% -> 21% of each run, Pallas kernels for 0% -> 0%
where the time goes in v1:
time: 664 us; the launch traced here: 661 us
  waiting for transfers between devices  274 us (41%)
  starting transfers between devices  165 us (25%)
  local copies, waits for them, and re-layouts  74.5 us (11%)
  matrix products  45.4 us (7%)
  other arithmetic  37 us (6%)
  loops' own time  25.3 us (4%)
  blocking collectives  25 us (4%)
  between operations  13.8 us (2%)
    all_to_all x7, starting transfers between devices, all_blocks(): lax.all_to_all(jnp.stack([blocks] * lax.axis_size(axes[k])), axes[k], 0, 0)  93.1 us
    psum x1, waiting for transfers between devices, per_device(): lax.psum(ff_terms.astype(jnp.bfloat16), 'head').astype(jnp.float32)  77.1 us
    psum x1, waiting for transfers between devices, per_device(): lax.psum(enc_terms.astype(jnp.bfloat16), 'head').astype(jnp.float32)  66.1 us
    psum x1, waiting for transfers between devices, per_device(): lax.psum(proc_terms.astype(jnp.bfloat16), 'head').astype(jnp.float32)  53.4 us
    all_to_all x3, starting transfers between devices, copy_for_each(): lax.all_to_all(jnp.broadcast_to(array[None], (size, *array.shape)), axis,...  31.6 us
    all_to_all x1, waiting for transfers between devices, summed_on_arrival(): blocks = lax.all_to_all(split_up(array, dim, size), axis, 0, 0, tiled=True)  29.2 us
    all_to_all x3, blocking collectives, all_blocks(): lax.all_to_all(jnp.stack([blocks] * lax.axis_size(axes[k])), axes[k], 0, 0)  25 us
    another operation x2, loops' own time, listed_attend(): result = lax.map(one_block, jnp.arange(rows // BLOCK, dtype=jnp.int32))  20.2 us
  transfers between devices with their start and end apart: 24, of which 12 were waited for; matrix products, arithmetic and copies ran while one was open for 21% of the time, Pallas kernels for 0%

profile of v1, /device:TPU:65, one launch (start us, length us, event | category | flops | bytes accessed | tf_op | source)
XLA Modules:
  0.0 660.6 jit_solution(7989126209290259015)
XLA Ops:
  8.2 44.2 %all-to-all-start.2 = ((bf16[16,1,3,32,128]{4,3,2,1,0:T(8,128)(2,1)}), bf16[16,1,3,32,128]{4,3,2,1,0:T(8,128)(2,1)S(1)}, u32[]{:S(2)}, u32[]{:S(2)}) async-start(bf16[16,1,3,32,128]{4,3,2,1,0:T(8,128)(2,1)} %stack.59), calls=%async_computation.2 | async-start | bytes 786432 | tf_op jit(solution)/shard_map/all_to_all | solution.py:27
  54.1 16.2 %all-to-all-done.2 = bf16[16,1,3,32,128]{4,3,2,1,0:T(8,128)(2,1)S(1)} async-done(((bf16[16,1,3,32,128]{4,3,2,1,0:T(8,128)(2,1)}), bf16[16,1,3,32,128]{4,3,2,1,0:T(8,128)(2,1)S(1)}, u32[]{:S(2)}, u32[]{:S(2)}) %all-to-all-start.2) | async-done | bytes 393248 | tf_op jit(solution)/shard_map/all_to_all | solution.py:27
  70.4 10.5 %all_to_all.70 = bf16[2,16,3,32,128]{4,3,2,1,0:T(8,128)(2,1)S(1)} all-to-all(bf16[2,16,3,32,128]{4,3,2,1,0:T(8,128)(2,1)S(1)} %pad_maximum_fusion.5), channel_id=1, replica_groups=mesh['members'=2,'band_0'=16,'band_1'=2,'head'=8] {'band_1'}, dimensions={0} | all-to-all | bytes 1572864 | tf_op jit(solution)/shard_map/all_to_all | solution.py:27
  81.7 6.7 %all-to-all-start.4 = ((bf16[32,128,32]{1,2,0:T(8,128)(2,1)}), bf16[32,128,32]{1,2,0:T(8,128)(2,1)S(1)}, u32[]{:S(2)}, u32[]{:S(2)}) async-start(bf16[32,128,32]{1,2,0:T(8,128)(2,1)} %broadcast_in_dim.140), calls=%async_computation.4 | async-start | bytes 524288 | tf_op jit(solution)/shard_map/all_to_all | solution.py:54
  97.1 7.8 %collective-permute-done.1 = bf16[2,512,128]{2,1,0:T(8,128)(2,1)S(1)} collective-permute-done((bf16[2,512,128]{2,1,0:T(8,128)(2,1)S(1)}, bf16[2,512,128]{2,1,0:T(8,128)(2,1)S(1)}, u32[]{:S(2)}, u32[]{:S(2)}) %collective-permute-start.1) | collective-permute-done | bytes 262176 | tf_op jit(solution)/shard_map/ppermute | solution.py:47
  105.1 5.3 all-to-all-done.4
  111.3 5.3 all-to-all-start.5
  117.2 38.0 %while.34 = (s32[]{:T(128)}, f32[4,128,128]{2,1,0:T(8,128)}, f32[4,128,2]{1,2,0:T(2,128)}, s32[4]{0:T(128)}, s32[4,8]{1,0:T(4,128)S(1)}, /*index=5*/s32[]{:T(128...) while((s32[]{:T(128)}, f32[4,128,128]{2,1,0:T(8,128)}, ...), condition=%wide.region_9.10_spmd, body=%wide.region_4.9_spmd.sunk | while | flops 69223264 | bytes 5784073 | solution.py:180
  165.3 12.5 %all-to-all-start.7 = ((bf16[32,128,32]{1,2,0:T(8,128)(2,1)}), bf16[32,128,32]{1,2,0:T(8,128)(2,1)S(1)}, u32[]{:S(2)}, u32[]{:S(2)}) async-start(bf16[32,128,32]{1,2,0:T(8,128)(2,1)} %broadcast_in_dim.141), calls=%async_computation.7 | async-start | bytes 524288 | tf_op jit(solution)/shard_map/all_to_all | solution.py:54
  178.7 66.1 %all-reduce.5.cloned.1.call-done = bf16[512,1024]{1,0:T(8,128)(2,1)} async-done(((bf16[512,1024]{1,0:T(8,128)(2,1)}), bf16[512,1024]{1,0:T(8,128)(2,1)}) %all-reduce.5.cloned.1.call-update) | async-done | bytes 1048592 | tf_op jit(solution)/shard_map/psum | solution.py:234
  247.9 13.1 %all-to-all-start.10 = ((bf16[16,1,512,32]{2,3,1,0:T(8,128)(2,1)}), bf16[16,1,512,32]{2,3,1,0:T(8,128)(2,1)}, u32[]{:S(2)}, u32[]{:S(2)}) async-start(bf16[16,1,512,32]{2,3,1,0:T(8,128)(2,1)} %stack.71), calls=%async_computation.10 | async-start | bytes 1048576 | tf_op jit(solution)/shard_map/all_to_all | solution.py:27
  262.9 10.5 %collective-permute-start.2 = (bf16[2,512,128]{2,1,0:T(8,128)(2,1)S(1)}, bf16[2,512,128]{2,1,0:T(8,128)(2,1)}, u32[]{:S(2)}, u32[]{:S(2)}) collective-permute-start(bf16[2,512,128]{2,1,0:T(8,128)(2,1)S(1)} %pad_maximum_fusion.10), channel_id=1, source_target_pairs={{0,24},{8,32},{16,40},{24,48},{32,56},{40,64},{48,72},{56,80},{64,... | collective-permute-start | bytes 786440 | tf_op jit(solution)/shard_map/ppermute | solution.py:66
  301.1 6.6 collective-permute-done.7
  309.3 11.7 %all-to-all-start.8 = ((bf16[16,1,32,512]{3,2,1,0:T(8,128)(2,1)}), bf16[16,1,32,512]{3,2,1,0:T(8,128)(2,1)S(1)}, u32[]{:S(2)}, u32[]{:S(2)}) async-start(bf16[16,1,32,512]{3,2,1,0:T(8,128)(2,1)} %stack.69), calls=%async_computation.8 | async-start | bytes 1048576 | tf_op jit(solution)/shard_map/all_to_all | solution.py:27
  321.7 54.7 %while.35 = (s32[]{:T(128)}, bf16[4,128,128]{2,1,0:T(8,128)(2,1)}, s32[4]{0:T(128)S(1)}, s32[]{:T(128)}, s32[16384]{0:T(1024)S(1)}, /*index=5*/s32[]{:T(128)}, s...) while((s32[]{:T(128)}, bf16[4,128,128]{2,1,0:T(8,128)(2,1)}, ...), condition=%wide.region_19.20_spmd, body=%wide.region_13.19_spmd.sunk | while | flops 211287568 | bytes 26145704 | solution.py:272
  394.2 11.5 %all-to-all-start = ((bf16[16,1,3,32,128]{4,3,2,1,0:T(8,128)(2,1)}), bf16[16,1,3,32,128]{4,3,2,1,0:T(8,128)(2,1)S(1)}, u32[]{:S(2)}, u32[]{:S(2)}) async-start(bf16[16,1,3,32,128]{4,3,2,1,0:T(8,128)(2,1)} %stack.57), calls=%async_computation | async-start | bytes 786432 | tf_op jit(solution)/shard_map/all_to_all | solution.py:27
  406.8 53.4 %all-reduce.7.cloned.1.call-done = bf16[512,1024]{1,0:T(8,128)(2,1)} async-done(((bf16[512,1024]{1,0:T(8,128)(2,1)}), bf16[512,1024]{1,0:T(8,128)(2,1)}) %all-reduce.7.cloned.1.call-update) | async-done | bytes 1048592 | tf_op jit(solution)/shard_map/psum | solution.py:276
  463.4 5.6 convolution_convert_fusion.7
  469.2 9.8 %all_to_all.72 = bf16[2,16,3,32,128]{4,3,2,1,0:T(8,128)(2,1)S(1)} all-to-all(bf16[2,16,3,32,128]{4,3,2,1,0:T(8,128)(2,1)S(1)} %pad_maximum_fusion.4), channel_id=1, replica_groups=mesh['members'=2,'band_0'=16,'band_1'=2,'head'=8] {'band_1'}, dimensions={0} | all-to-all | bytes 1572864 | tf_op jit(solution)/shard_map/all_to_all | solution.py:27
  480.0 77.1 %all-reduce.9.cloned.1.call-done = bf16[512,1024]{1,0:T(8,128)(2,1)} async-done(((bf16[512,1024]{1,0:T(8,128)(2,1)}), bf16[512,1024]{1,0:T(8,128)(2,1)}) %all-reduce.9.cloned.1.call-update) | async-done | bytes 1048592 | tf_op jit(solution)/shard_map/psum | solution.py:285
  561.0 7.6 %collective-permute-start.9 = (bf16[2,512,128]{2,1,0:T(8,128)(2,1)S(1)}, bf16[2,512,128]{2,1,0:T(8,128)(2,1)S(1)}, u32[]{:S(2)}, u32[]{:S(2)}) collective-permute-start(bf16[2,512,128]{2,1,0:T(8,128)(2,1)S(1)} %pad_maximum_fusion.11), channel_id=1, source_target_pairs={{8,0},{16,8},{24,16},{32,24},{40,32},{48,40},{56,48},{64,56},{72,6... | collective-permute-start | bytes 786440 | tf_op jit(solution)/shard_map/ppermute | solution.py:47
  572.5 12.4 %all-to-all-start.12 = ((bf16[32,128,32]{1,2,0:T(8,128)(2,1)}), bf16[32,128,32]{1,2,0:T(8,128)(2,1)S(1)}, u32[]{:S(2)}, u32[]{:S(2)}) async-start(bf16[32,128,32]{1,2,0:T(8,128)(2,1)} %broadcast_in_dim.142), calls=%async_computation.12 | async-start | bytes 524288 | tf_op jit(solution)/shard_map/all_to_all | solution.py:54
  585.7 31.9 %while.36 = (s32[]{:T(128)}, bf16[4,128,128]{2,1,0:T(8,128)(2,1)S(1)}, s32[4]{0:T(128)S(1)}, s32[4,8]{1,0:T(4,128)S(1)}, s32[]{:T(128)}, /*index=5*/s32[4]{0:T(1...) while((s32[]{:T(128)}, ...), condition=%wide.region_31.32_spmd, body=%wide.region_26.31_spmd.sunk | while | flops 69812832 | bytes 5553661 | solution.py:180
  623.1 29.2 %all-to-all-done.13 = bf16[8,64,1024]{2,1,0:T(8,128)(2,1)S(1)} async-done(((bf16[8,64,1024]{2,1,0:T(8,128)(2,1)}), bf16[8,64,1024]{2,1,0:T(8,128)(2,1)S(1)}, u32[]{:S(2)}, u32[]{:S(2)}) %all-to-all-start.13) | async-done | bytes 1048608 | tf_op jit(solution)/shard_map/all_to_all | solution.py:77
  (387 shorter events, 198.2 us)
Async XLA Ops:
  8.2 62.1 %all-to-all-start.2 = ((bf16[16,1,3,32,128]{4,3,2,1,0:T(8,128)(2,1)}), bf16[16,1,3,32,128]{4,3,2,1,0:T(8,128)(2,1)S(1)}, u32[]{:S(2)}, u32[]{:S(2)}) async-start(bf16[16,1,3,32,128]{4,3,2,1,0:T(8,128)(2,1)} %stack.59), calls=%async_computation.2 | async-start | bytes 786432 | tf_op jit(solution)/shard_map/all_to_all | solution.py:27
  81.7 28.7 %all-to-all-start.4 = ((bf16[32,128,32]{1,2,0:T(8,128)(2,1)}), bf16[32,128,32]{1,2,0:T(8,128)(2,1)S(1)}, u32[]{:S(2)}, u32[]{:S(2)}) async-start(bf16[32,128,32]{1,2,0:T(8,128)(2,1)} %broadcast_in_dim.140), calls=%async_computation.4 | async-start | bytes 524288 | tf_op jit(solution)/shard_map/all_to_all | solution.py:54
  89.6 15.4 %collective-permute-start.1 = (bf16[2,512,128]{2,1,0:T(8,128)(2,1)S(1)}, bf16[2,512,128]{2,1,0:T(8,128)(2,1)S(1)}, u32[]{:S(2)}, u32[]{:S(2)}) collective-permute-start(bf16[2,512,128]{2,1,0:T(8,128)(2,1)S(1)} %pad_maximum_fusion.9), channel_id=1, source_target_pairs={{8,0},{16,8},{24,16},{32,24},{40,32},{48,40},{56,48},{64,56},{72,6... | collective-permute-start | bytes 786440 | tf_op jit(solution)/shard_map/ppermute | solution.py:47
  92.2 12.7 %collective-permute-start = (bf16[2,512,128]{2,1,0:T(8,128)(2,1)S(1)}, bf16[2,512,128]{2,1,0:T(8,128)(2,1)S(1)}, u32[]{:S(2)}, u32[]{:S(2)}) collective-permute-start(bf16[2,512,128]{2,1,0:T(8,128)(2,1)S(1)} %pad_maximum_fusion.9), channel_id=1, source_target_pairs={{0,8},{8,16},{16,24},{24,32},{32,40},{40,48},{48,56},{56,64},{64,7... | collective-permute-start | bytes 786440 | tf_op jit(solution)/shard_map/ppermute | solution.py:44
  111.3 47.4 %all-to-all-start.5 = ((bf16[16,1,3,32,128]{4,3,2,1,0:T(8,128)(2,1)}), bf16[16,1,3,32,128]{4,3,2,1,0:T(8,128)(2,1)}, u32[]{:S(2)}, u32[]{:S(2)}) async-start(bf16[16,1,3,32,128]{4,3,2,1,0:T(8,128)(2,1)} %stack.64), calls=%async_computation.5 | async-start | bytes 786432 | tf_op jit(solution)/shard_map/all_to_all | solution.py:27
  116.6 128.3 %all-reduce.5.cloned.1.call-start = ((), (), s32[]{:S(2)}) async-start(), calls=%async_computation.14 | async-start | bytes 2097152 | tf_op jit(solution)/shard_map/psum | solution.py:234
  165.3 81.7 %all-to-all-start.7 = ((bf16[32,128,32]{1,2,0:T(8,128)(2,1)}), bf16[32,128,32]{1,2,0:T(8,128)(2,1)S(1)}, u32[]{:S(2)}, u32[]{:S(2)}) async-start(bf16[32,128,32]{1,2,0:T(8,128)(2,1)} %broadcast_in_dim.141), calls=%async_computation.7 | async-start | bytes 524288 | tf_op jit(solution)/shard_map/all_to_all | solution.py:54
  247.9 60.5 %all-to-all-start.10 = ((bf16[16,1,512,32]{2,3,1,0:T(8,128)(2,1)}), bf16[16,1,512,32]{2,3,1,0:T(8,128)(2,1)}, u32[]{:S(2)}, u32[]{:S(2)}) async-start(bf16[16,1,512,32]{2,3,1,0:T(8,128)(2,1)} %stack.71), calls=%async_computation.10 | async-start | bytes 1048576 | tf_op jit(solution)/shard_map/all_to_all | solution.py:27
  262.9 23.9 %collective-permute-start.2 = (bf16[2,512,128]{2,1,0:T(8,128)(2,1)S(1)}, bf16[2,512,128]{2,1,0:T(8,128)(2,1)}, u32[]{:S(2)}, u32[]{:S(2)}) collective-permute-start(bf16[2,512,128]{2,1,0:T(8,128)(2,1)S(1)} %pad_maximum_fusion.10), channel_id=1, source_target_pairs={{0,24},{8,32},{16,40},{24,48},{32,56},{40,64},{48,72},{56,80},{64,... | collective-permute-start | bytes 786440 | tf_op jit(solution)/shard_map/ppermute | solution.py:66
  273.5 20.1 %collective-permute-start.3 = (bf16[2,512,128]{2,1,0:T(8,128)(2,1)S(1)}, bf16[2,512,128]{2,1,0:T(8,128)(2,1)S(1)}, u32[]{:S(2)}, u32[]{:S(2)}) collective-permute-start(bf16[2,512,128]{2,1,0:T(8,128)(2,1)S(1)} %pad_maximum_fusion.10), channel_id=1, source_target_pairs={{0,16},{8,24},{16,32},{24,40},{32,48},{40,56},{48,64},{56,72},{64,... | collective-permute-start | bytes 786440 | tf_op jit(solution)/shard_map/ppermute | solution.py:66
  276.0 22.2 %collective-permute-start.4 = (bf16[2,512,128]{2,1,0:T(8,128)(2,1)S(1)}, bf16[2,512,128]{2,1,0:T(8,128)(2,1)S(1)}, u32[]{:S(2)}, u32[]{:S(2)}) collective-permute-start(bf16[2,512,128]{2,1,0:T(8,128)(2,1)S(1)} %pad_maximum_fusion.10), channel_id=1, source_target_pairs={{0,8},{8,16},{16,24},{24,32},{32,40},{40,48},{48,56},{56,64},{64,7... | collective-permute-start | bytes 786440 | tf_op jit(solution)/shard_map/ppermute | solution.py:66
  278.1 21.6 %collective-permute-start.5 = (bf16[2,512,128]{2,1,0:T(8,128)(2,1)S(1)}, bf16[2,512,128]{2,1,0:T(8,128)(2,1)S(1)}, u32[]{:S(2)}, u32[]{:S(2)}) collective-permute-start(bf16[2,512,128]{2,1,0:T(8,128)(2,1)S(1)} %pad_maximum_fusion.10), channel_id=1, source_target_pairs={{8,0},{16,8},{24,16},{32,24},{40,32},{48,40},{56,48},{64,56},{72,6... | collective-permute-start | bytes 786440 | tf_op jit(solution)/shard_map/ppermute | solution.py:66
  280.6 19.8 %collective-permute-start.6 = (bf16[2,512,128]{2,1,0:T(8,128)(2,1)S(1)}, bf16[2,512,128]{2,1,0:T(8,128)(2,1)S(1)}, u32[]{:S(2)}, u32[]{:S(2)}) collective-permute-start(bf16[2,512,128]{2,1,0:T(8,128)(2,1)S(1)} %pad_maximum_fusion.10), channel_id=1, source_target_pairs={{16,0},{24,8},{32,16},{40,24},{48,32},{56,40},{64,48},{72,56},{80,... | collective-permute-start | bytes 786440 | tf_op jit(solution)/shard_map/ppermute | solution.py:66
  286.8 20.9 %collective-permute-start.7 = (bf16[2,512,128]{2,1,0:T(8,128)(2,1)S(1)}, bf16[2,512,128]{2,1,0:T(8,128)(2,1)S(1)}, u32[]{:S(2)}, u32[]{:S(2)}) collective-permute-start(bf16[2,512,128]{2,1,0:T(8,128)(2,1)S(1)} %pad_maximum_fusion.10), channel_id=1, source_target_pairs={{24,0},{32,8},{40,16},{48,24},{56,32},{64,40},{72,48},{80,56},{88,... | collective-permute-start | bytes 786440 | tf_op jit(solution)/shard_map/ppermute | solution.py:66
  309.3 71.9 %all-to-all-start.8 = ((bf16[16,1,32,512]{3,2,1,0:T(8,128)(2,1)}), bf16[16,1,32,512]{3,2,1,0:T(8,128)(2,1)S(1)}, u32[]{:S(2)}, u32[]{:S(2)}) async-start(bf16[16,1,32,512]{3,2,1,0:T(8,128)(2,1)} %stack.69), calls=%async_computation.8 | async-start | bytes 1048576 | tf_op jit(solution)/shard_map/all_to_all | solution.py:27
  321.0 139.2 %all-reduce.7.cloned.1.call-start = ((), (), s32[]{:S(2)}) async-start(), calls=%async_computation.15 | async-start | bytes 2097152 | tf_op jit(solution)/shard_map/psum | solution.py:276
  382.0 5.9 all-to-all-start.11
  387.9 5.5 all-to-all-start.9
  394.2 74.9 %all-to-all-start = ((bf16[16,1,3,32,128]{4,3,2,1,0:T(8,128)(2,1)}), bf16[16,1,3,32,128]{4,3,2,1,0:T(8,128)(2,1)S(1)}, u32[]{:S(2)}, u32[]{:S(2)}) async-start(bf16[16,1,3,32,128]{4,3,2,1,0:T(8,128)(2,1)} %stack.57), calls=%async_computation | async-start | bytes 786432 | tf_op jit(solution)/shard_map/all_to_all | solution.py:27
  405.7 151.4 %all-reduce.9.cloned.1.call-start = ((), (), s32[]{:S(2)}) async-start(), calls=%async_computation.16 | async-start | bytes 2097152 | tf_op jit(solution)/shard_map/psum | solution.py:285
  561.0 24.6 %collective-permute-start.9 = (bf16[2,512,128]{2,1,0:T(8,128)(2,1)S(1)}, bf16[2,512,128]{2,1,0:T(8,128)(2,1)S(1)}, u32[]{:S(2)}, u32[]{:S(2)}) collective-permute-start(bf16[2,512,128]{2,1,0:T(8,128)(2,1)S(1)} %pad_maximum_fusion.11), channel_id=1, source_target_pairs={{8,0},{16,8},{24,16},{32,24},{40,32},{48,40},{56,48},{64,56},{72,6... | collective-permute-start | bytes 786440 | tf_op jit(solution)/shard_map/ppermute | solution.py:47
  568.6 17.0 %collective-permute-start.8 = (bf16[2,512,128]{2,1,0:T(8,128)(2,1)S(1)}, bf16[2,512,128]{2,1,0:T(8,128)(2,1)S(1)}, u32[]{:S(2)}, u32[]{:S(2)}) collective-permute-start(bf16[2,512,128]{2,1,0:T(8,128)(2,1)S(1)} %pad_maximum_fusion.11), channel_id=1, source_target_pairs={{0,8},{8,16},{16,24},{24,32},{32,40},{40,48},{48,56},{56,64},{64,7... | collective-permute-start | bytes 786440 | tf_op jit(solution)/shard_map/ppermute | solution.py:44
  572.5 45.2 %all-to-all-start.12 = ((bf16[32,128,32]{1,2,0:T(8,128)(2,1)}), bf16[32,128,32]{1,2,0:T(8,128)(2,1)S(1)}, u32[]{:S(2)}, u32[]{:S(2)}) async-start(bf16[32,128,32]{1,2,0:T(8,128)(2,1)} %broadcast_in_dim.142), calls=%async_computation.12 | async-start | bytes 524288 | tf_op jit(solution)/shard_map/all_to_all | solution.py:54
  619.1 33.1 %all-to-all-start.13 = ((bf16[8,64,1024]{2,1,0:T(8,128)(2,1)}), bf16[8,64,1024]{2,1,0:T(8,128)(2,1)S(1)}, u32[]{:S(2)}, u32[]{:S(2)}) async-start(bf16[8,64,1024]{2,1,0:T(8,128)(2,1)} %bitcast.83), calls=%async_computation.13 | async-start | bytes 2097152 | tf_op jit(solution)/shard_map/all_to_all | solution.py:77
  (36 other events, 424.5 us)
Sparse Core Ops, SparseCore 0:
  158.8 85.9 all-reduce.4
  379.0 81.1 all-reduce.6
  469.2 87.7 all-reduce.8
